TPU v7x, 32 devices: a whole 2x2x4 slice. The times are simulated.
32 devices in a mesh: expert: 4 (over y, x), tensor: 4 (over z), dp: 2 (over core).
Axes of the slice: x: 2, y: 2, z: 4, core: 2. Of those that a mesh axis runs over, the one named last changes fastest.
Arguments:
- x_real: bfloat16 [2048, 2048], P(('expert', 'dp'), 'tensor'), may hold values from -6 to 6
- routes_real: int32 [2048, 2], P(('expert', 'dp')), may hold values from 0 to 3, all different within a row; in each aligned block of 256 rows (0 to 255, 256 to 511, ...) at most 128 rows name the same one
- gates_real: float32 [2048, 2], P(('expert', 'dp')), may hold values from 0.2 to 1
- up_real: bfloat16 [4, 2048, 8192], P('expert', None, 'tensor'), may hold values from -0.125 to 0.125
- down_real: bfloat16 [4, 8192, 2048], P('expert', 'tensor'), may hold values from -0.0625 to 0.0625
- x_fake: bfloat16 [2048, 2048], P(('expert', 'dp'), 'tensor'), may hold values from -6 to 6
- routes_fake: int32 [2048, 2], P(('expert', 'dp')), may hold values from 0 to 3, all different within a row; in each aligned block of 256 rows (0 to 255, 256 to 511, ...) at most 128 rows name the same one
- gates_fake: float32 [2048, 2], P(('expert', 'dp')), may hold values from 0.2 to 1
- cotangent: bfloat16 [2048, 2048], P(('expert', 'dp'), 'tensor'), may hold values from -6 to 6
- up_fake: bfloat16 [4, 2048, 8192], P('expert', None, 'tensor'), may hold values from -0.125 to 0.125
- down_fake: bfloat16 [4, 8192, 2048], P('expert', 'tensor'), may hold values from -0.0625 to 0.0625
Outputs:
- real_out: bfloat16 [2048, 2048], P(('expert', 'dp'), 'tensor')
- grad_up: bfloat16 [4, 2048, 8192], P('expert', 'dp', 'tensor')
- grad_down: bfloat16 [4, 8192, 2048], P('expert', 'tensor', 'dp')
Inputs may be any that keep to these rules, and one draw needn't show every extreme that they name: `routes_real`: each row names 2 different experts. In the 256 rows of one index of expert and dp no expert is named more than 128 times, and that bound is reached. `routes_fake`: each row names 2 different experts. In the 256 rows of one index of expert and dp no expert is named more than 128 times, and that bound is reached.
All inputs are finite; a program needn't handle non-finite values.
Results may differ from a plain program's by a relative error of at most 0.0058.
Values may be sent and summed in bfloat16 or wider, within the bound.
A program may use at most 192 MiB of HBM per device.

v0:
```python
import functools

import jax
import jax.numpy as jnp
from jax import lax
from jax.experimental import pallas as pl
from jax.experimental.pallas import tpu as pltpu
from jax.sharding import PartitionSpec as P

slope_const = 0.7978845608028654
cubic_coef = 0.044715
MESH = pl.DeviceIdType.MESH
F32 = jnp.float32
BF16 = jnp.bfloat16
LAG = 2


def dot32(left, right, dims=((1,), (0,))):
    return lax.dot_general(left, right, (dims, ((), ())), preferred_element_type=F32)


def tanh_of(value):
    return jnp.tanh(slope_const * (value + cubic_coef * value * value * value))


def gelu_from(value, inner):
    return 0.5 * value * (1.0 + inner)


def slope_from(value, inner):
    return 0.5 * (1.0 + inner) + 0.5 * value * (1.0 - inner * inner) * slope_const * (
        1.0 + 3.0 * cubic_coef * value * value
    )


def moe_kernel(
    experts,
    tensors,
    routes_real,
    gates_real,
    routes_fake,
    gates_fake,
    x_real,
    x_fake,
    cotangent,
    up_real,
    down_real,
    up_fake,
    down_fake,
    real_out,
    grad_up,
    grad_down,
    whole,
    sendbuf,
    rows,
    acc0,
    acc1,
    weight0,
    weight1,
    pick,
    pick_k,
    gate,
    act,
    dpre,
    other_x,
    other_d,
    partial,
    from_left,
    from_right,
    final,
    ret_send,
    returned,
    stage_up,
    stage_down,
    in_sem,
    w_sem,
    z_recv,
    z_right,
    z_left,
    x_send,
    x_recv,
    d_send,
    d_recv,
    big_send,
    big_recv,
    rsr_send,
    rsr_recv,
    rsl_send,
    rsl_recv,
    ret_sems,
    up_sem,
    down_sem,
):
    E, T = experts, tensors
    top, tokens = routes_real.shape
    cap = tokens // 2
    total = E * cap
    part = x_real.shape[1]
    FF = act.shape[1]
    NT = stage_up.shape[2]
    tiles = FF // NT
    half = T // 2
    e = lax.axis_index("expert")
    t = lax.axis_index("tensor")
    d = lax.axis_index("dp")
    last = T - 1

    barrier = pltpu.get_barrier_semaphore()
    for s in range(1, E):
        pl.semaphore_signal(barrier, inc=1, device_id={"expert": e ^ s}, device_id_type=MESH)
    pl.semaphore_signal(barrier, inc=1, device_id={"dp": 1 - d}, device_id_type=MESH)

    @pl.when(t > 0)
    def _():
        pl.semaphore_signal(barrier, inc=1, device_id={"tensor": t - 1}, device_id_type=MESH)

    @pl.when(t < last)
    def _():
        pl.semaphore_signal(barrier, inc=1, device_id={"tensor": t + 1}, device_id_type=MESH)

    own_in = [
        pltpu.make_async_copy(src, whole.at[a * T + t], in_sem.at[a])
        for a, src in enumerate((x_real, x_fake, cotangent))
    ]
    for copy in own_in:
        copy.start()

    def load(src, dst, k):
        return pltpu.make_async_copy(src.at[0], dst, w_sem.at[k])

    load(up_real, weight0, 0).start()
    load(down_real, weight1, 1).start()

    pl.semaphore_wait(barrier, E + jnp.minimum(t, 1) + jnp.minimum(last - t, 1))

    def z_copy(i, q, right):
        a = i // T
        k = a * T + q
        return pltpu.make_async_remote_copy(
            src_ref=whole.at[k],
            dst_ref=whole.at[k],
            send_sem=(z_right if right else z_left).at[k],
            recv_sem=z_recv.at[k],
            device_id={"tensor": t + 1 if right else t - 1},
            device_id_type=MESH,
        )

    near = jnp.minimum(t, last - t)

    def source(p):
        step = (p + 1) // 2
        close = jnp.where(p % 2 == 1, t - step, t + step)
        beyond = jnp.where(t < last - t, t + p - near, t - p + near)
        return jnp.where(p <= 2 * near, close, beyond)

    def gather_step(i):
        q = source(i % T)

        @pl.when(q != t)
        def _():
            z_copy(i, q, True).wait_recv()

        @pl.when(jnp.logical_and(q <= t, t < last))
        def _():
            z_copy(i, q, True).start()

        @pl.when(jnp.logical_and(q >= t, t > 0))
        def _():
            z_copy(i, q, False).start()

    def x_copies(k):
        return [
            pltpu.make_async_remote_copy(
                src_ref=sendbuf.at[k, pl.ds((s - 1) * cap, cap)],
                dst_ref=rows.at[k, pl.ds(s * cap, cap)],
                send_sem=x_send.at[k],
                recv_sem=x_recv.at[k],
                device_id={"expert": e ^ s},
                device_id_type=MESH,
            )
            for s in range(1, E)
        ]

    def x_all(k):
        return pltpu.make_async_remote_copy(
            src_ref=sendbuf.at[k],
            dst_ref=rows.at[k, pl.ds(cap, total - cap)],
            send_sem=x_send.at[k],
            recv_sem=x_recv.at[k],
            device_id={"expert": e ^ 1},
            device_id_type=MESH,
        )

    def dispatch_step(i):
        a = i // T
        k = a * T + source(i % T)
        which = jnp.minimum(a, 1)
        picked = (dot32(pick[which], whole[k]) * gate[a]).astype(BF16)
        rows[k, 0:cap] = picked[0:cap]
        sendbuf[k] = picked[cap:total]
        for copy in x_copies(k):
            copy.start()

    def feed(i):
        gather_step(i)
        dispatch_step(i)

    own_in[0].wait()
    gather_step(0)

    square = (tokens, tokens)
    down_at = lax.broadcasted_iota(jnp.int32, square, 0)
    along = lax.broadcasted_iota(jnp.int32, square, 1)
    eye = down_at == along
    upper = (down_at < along).astype(BF16)
    labels_high = max(8, E)
    labels = lax.broadcasted_iota(jnp.int32, (labels_high, tokens), 0).astype(F32)
    slot_rows = lax.broadcasted_iota(jnp.int32, (total, tokens), 0).astype(F32)

    def stand_up(row):
        return jnp.sum(jnp.where(eye, row, 0.0), axis=1, keepdims=True)

    def positions(routes):
        names = [routes[k : k + 1, :].astype(F32) for k in range(top)]
        places = [(routes[k : k + 1, :] ^ e).astype(F32) for k in range(top)]
        hits = jnp.zeros((labels_high, tokens), F32)
        for name in names:
            hits = hits + (labels == name).astype(F32)
        before = dot32(hits.astype(BF16), upper)
        found = []
        for name, place in zip(names, places):
            slot = jnp.sum(jnp.where(labels == name, before, 0.0), axis=0, keepdims=True)
            found.append(place * cap + slot)
        return found

    chosen = jnp.zeros((total, tokens), BF16)
    for k, where in enumerate(positions(routes_real)):
        mask = (slot_rows == where).astype(F32).astype(BF16)
        pick_k[k] = mask
        chosen = chosen + mask
    pick[0] = chosen
    gate[0] = jnp.ones((total, 1), F32)
    dispatch_step(0)
    gate[1] = jnp.ones((total, 1), F32)
    chosen = jnp.zeros((total, tokens), BF16)
    gated = jnp.zeros((total, tokens), F32)
    for k, where in enumerate(positions(routes_fake)):
        mask = slot_rows == where
        chosen = chosen + mask.astype(F32).astype(BF16)
        gated = jnp.where(mask, gates_fake[k : k + 1, :], gated)
    pick[1] = chosen
    gate[2] = jnp.sum(gated, axis=1, keepdims=True)
    own_in[1].wait()
    own_in[2].wait()
    for i in range(1, LAG):
        feed(jnp.int32(i))

    def tile_at(n):
        return pl.ds(pl.multiple_of(n * NT, NT), NT)

    def part_at(q):
        return pl.ds(pl.multiple_of(q * part, part), part)

    def clear(target):
        @pl.loop(0, tiles)
        def _(n):
            target[:, tile_at(n)] = jnp.zeros((total, NT), F32)

    clear(acc0)
    load(up_real, weight0, 0).wait()

    @pl.loop(0, T)
    def _(p):
        q = source(p)
        x_all(q).wait_recv()

        @pl.loop(0, tiles)
        def _(n):
            acc0[:, tile_at(n)] += dot32(rows[q], weight0[part_at(q), tile_at(n)])

        feed(p + LAG)

    load(up_fake, weight0, 2).start()

    @pl.loop(0, tiles)
    def _(n):
        value = acc0[:, tile_at(n)]
        dpre[0:total, tile_at(n)] = gelu_from(value, tanh_of(value)).astype(BF16)

    load(down_real, weight1, 1).wait()

    @pl.loop(0, T)
    def _(c):
        partial[c] = dot32(dpre[0:total], weight1[:, part_at(c)]).astype(BF16)

    load(down_fake, weight1, 3).start()

    def rs_right(c, first):
        return pltpu.make_async_remote_copy(
            src_ref=partial.at[c] if first else from_left.at[c],
            dst_ref=from_left.at[c],
            send_sem=rsr_send.at[c],
            recv_sem=rsr_recv.at[c],
            device_id={"tensor": t + 1},
            device_id_type=MESH,
        )

    def rs_left(c, first):
        return pltpu.make_async_remote_copy(
            src_ref=partial.at[c] if first else from_right.at[c],
            dst_ref=from_right.at[c],
            send_sem=rsl_send.at[c],
            recv_sem=rsl_recv.at[c],
            device_id={"tensor": t - 1},
            device_id_type=MESH,
        )

    def rs_round(h):
        c_right = last - h + t
        go_right = jnp.logical_and(h >= t, t < last)

        @pl.when(jnp.logical_and(go_right, t == 0))
        def _():
            rs_right(c_right, True).start()

        @pl.when(jnp.logical_and(go_right, t > 0))
        def _():
            rs_right(c_right, False).wait_recv()
            joined = from_left[c_right].astype(F32) + partial[c_right].astype(F32)
            from_left[c_right] = joined.astype(BF16)
            rs_right(c_right, False).start()

        c_left = h - (last - t)
        go_left = jnp.logical_and(h >= last - t, t > 0)

        @pl.when(jnp.logical_and(go_left, t == last))
        def _():
            rs_left(c_left, True).start()

        @pl.when(jnp.logical_and(go_left, t < last))
        def _():
            rs_left(c_left, False).wait_recv()
            joined = from_right[c_left].astype(F32) + partial[c_left].astype(F32)
            from_right[c_left] = joined.astype(BF16)
            rs_left(c_left, False).start()

    def ret_copies():
        return [
            pltpu.make_async_remote_copy(
                src_ref=ret_send.at[pl.ds(s * cap, cap)],
                dst_ref=returned.at[pl.ds(s * cap, cap)],
                send_sem=ret_sems.at[0],
                recv_sem=ret_sems.at[1],
                device_id={"expert": e ^ s},
                device_id_type=MESH,
            )
            for s in range(1, E)
        ]

    def ret_all():
        return pltpu.make_async_remote_copy(
            src_ref=ret_send.at[pl.ds(cap, total - cap)],
            dst_ref=returned.at[pl.ds(cap, total - cap)],
            send_sem=ret_sems.at[0],
            recv_sem=ret_sems.at[1],
            device_id={"expert": e ^ 1},
            device_id_type=MESH,
        )

    def rs_final():
        final[...] = partial[t].astype(F32)

        @pl.when(t > 0)
        def _():
            rs_right(t, False).wait_recv()
            final[...] += from_left[t].astype(F32)

        @pl.when(t < last)
        def _():
            rs_left(t, False).wait_recv()
            final[...] += from_right[t].astype(F32)

        summed = final[...].astype(BF16)
        ret_send[...] = summed
        returned[0:cap] = summed[0:cap]
        for copy in ret_copies():
            copy.start()

    def rs_slot(j):
        h = j // 2

        @pl.when(jnp.logical_and(j % 2 == 0, jnp.logical_and(j > 0, h < last)))
        def _():
            rs_round(h)

        @pl.when(j == 2 * last)
        def _():
            rs_final()

    rs_round(jnp.int32(0))

    def half_of(q):
        return q // half

    def swap(a, q, target):
        k = a * T + q
        other = q - (1 - d) * half
        return pltpu.make_async_remote_copy(
            src_ref=rows.at[k],
            dst_ref=target.at[other],
            send_sem=d_send.at[(a - 1) * half + other],
            recv_sem=d_recv.at[(a - 1) * half + other],
            device_id={"dp": 1 - d},
            device_id_type=MESH,
        )

    clear(acc1)
    load(up_fake, weight0, 2).wait()

    @pl.loop(0, T)
    def _(p):
        q = source(p)
        x_all(T + q).wait_recv()

        @pl.when(half_of(q) != d)
        def _():
            swap(1, q, other_x).start()

        @pl.loop(0, tiles)
        def _(n):
            acc1[:, tile_at(n)] += dot32(rows[T + q], weight0[part_at(q), tile_at(n)])

        feed(T + p + LAG)
        rs_slot(p)

    @pl.loop(0, tiles)
    def _(n):
        value = acc1[:, tile_at(n)]
        inner = tanh_of(value)
        act[0:total, tile_at(n)] = gelu_from(value, inner).astype(BF16)
        acc1[:, tile_at(n)] = slope_from(value, inner)

    def across(buffer, k):
        return pltpu.make_async_remote_copy(
            src_ref=buffer.at[pl.ds(0, total)],
            dst_ref=buffer.at[pl.ds(total, total)],
            send_sem=big_send.at[k],
            recv_sem=big_recv.at[k],
            device_id={"dp": 1 - d},
            device_id_type=MESH,
        )

    clear(acc0)
    across(act, 0).start()
    load(down_fake, weight1, 3).wait()

    @pl.loop(0, T)
    def _(p):
        q = source(p)
        x_all(2 * T + q).wait_recv()

        @pl.when(half_of(q) != d)
        def _():
            swap(2, q, other_d).start()

        @pl.loop(0, tiles)
        def _(n):
            acc0[:, tile_at(n)] += dot32(
                rows[2 * T + q], weight1[tile_at(n), part_at(q)], ((1,), (1,))
            )

        @pl.when(p + LAG < T)
        def _():
            feed(2 * T + p + LAG)

        rs_slot(T + p)

    @pl.loop(0, tiles)
    def _(n):
        dpre[0:total, tile_at(n)] = (acc0[:, tile_at(n)] * acc1[:, tile_at(n)]).astype(BF16)

    across(dpre, 1).start()

    def other_in(a, j, target):
        return pltpu.make_async_remote_copy(
            src_ref=rows.at[a * T + j],
            dst_ref=target.at[j],
            send_sem=d_send.at[(a - 1) * half + j],
            recv_sem=d_recv.at[(a - 1) * half + j],
            device_id={"dp": 1 - d},
            device_id_type=MESH,
        )

    @pl.loop(0, half)
    def _(j):
        other_in(1, j, other_x).wait_recv()
        other_in(2, j, other_d).wait_recv()

    across(act, 0).wait_recv()
    base = d * half

    def put_down(j, n):
        slot = (j * tiles + n) % 2
        return pltpu.make_async_copy(
            stage_down.at[slot], grad_down.at[0, tile_at(n), part_at(j)], down_sem.at[slot]
        )

    def put_up(j, n):
        slot = (j * tiles + n) % 2
        return pltpu.make_async_copy(
            stage_up.at[slot], grad_up.at[0, part_at(j), tile_at(n)], up_sem.at[slot]
        )

    @pl.loop(0, half * tiles)
    def _(w):
        j = w // tiles
        n = w % tiles

        @pl.when(w >= 2)
        def _():
            put_down(j, n).wait()

        tile = dot32(act[0:total, tile_at(n)], rows[2 * T + base + j], ((0,), (0,)))
        tile = tile + dot32(act[total : 2 * total, tile_at(n)], other_d[j], ((0,), (0,)))
        stage_down[w % 2] = tile.astype(BF16)
        put_down(j, n).start()

    across(dpre, 1).wait_recv()

    @pl.loop(0, half * tiles)
    def _(w):
        j = w // tiles
        n = w % tiles

        @pl.when(w >= 2)
        def _():
            put_up(j, n).wait()

        tile = dot32(rows[T + base + j], dpre[0:total, tile_at(n)], ((0,), (0,)))
        tile = tile + dot32(other_x[j], dpre[total : 2 * total, tile_at(n)], ((0,), (0,)))
        stage_up[w % 2] = tile.astype(BF16)
        put_up(j, n).start()

    ret_all().wait_recv()
    out = jnp.zeros((tokens, part), F32)
    for k in range(top):
        back = dot32(pick_k[k], returned[...], ((0,), (0,)))
        out = out + stand_up(gates_real[k : k + 1, :]) * back
    real_out[...] = out.astype(BF16)

    for w in range(max(0, half * tiles - 2), half * tiles):
        put_down(w // tiles, w % tiles).wait()
        put_up(w // tiles, w % tiles).wait()

    @pl.loop(0, 3 * T)
    def _(k):
        x_all(k).wait_send()
        q = k % T

        @pl.when(jnp.logical_and(q <= t, t < last))
        def _():
            z_copy(k, q, True).wait_send()

        @pl.when(jnp.logical_and(q >= t, t > 0))
        def _():
            z_copy(k, q, False).wait_send()

    @pl.loop(0, half)
    def _(j):
        other_in(1, j, other_x).wait_send()
        other_in(2, j, other_d).wait_send()

    across(act, 0).wait_send()
    across(dpre, 1).wait_send()
    ret_all().wait_send()

    @pl.loop(0, T)
    def _(c):
        @pl.when(c > t)
        def _():
            rs_right(c, False).wait_send()

        @pl.when(c < t)
        def _():
            rs_left(c, False).wait_send()


def on_device(
    x_real,
    routes_real,
    gates_real,
    up_real,
    down_real,
    x_fake,
    routes_fake,
    gates_fake,
    cotangent,
    up_fake,
    down_fake,
):
    E = lax.axis_size("expert")
    T = lax.axis_size("tensor")
    tokens, part = x_real.shape
    top = routes_real.shape[1]
    cap = tokens // 2
    total = E * cap
    D = up_real.shape[1]
    FF = up_real.shape[2]
    NT = min(512, FF)
    half = T // 2
    vmem = pl.BlockSpec(memory_space=pltpu.VMEM)
    hbm = pl.BlockSpec(memory_space=pl.ANY)
    dma = pltpu.SemaphoreType.DMA
    return pl.pallas_call(
        functools.partial(moe_kernel, E, T),
        name="moe",
        out_shape=(
            jax.ShapeDtypeStruct((tokens, part), BF16),
            jax.ShapeDtypeStruct((1, D // 2, FF), BF16),
            jax.ShapeDtypeStruct((1, FF, D // 2), BF16),
        ),
        in_specs=[vmem] * 4 + [hbm] * 7,
        out_specs=(vmem, hbm, hbm),
        scratch_shapes=[
            pltpu.VMEM((3 * T, tokens, part), BF16),
            pltpu.VMEM((3 * T, total - cap, part), BF16),
            pltpu.VMEM((3 * T, total, part), BF16),
            pltpu.VMEM((total, FF), F32),
            pltpu.VMEM((total, FF), F32),
            pltpu.VMEM((D, FF), BF16),
            pltpu.VMEM((FF, D), BF16),
            pltpu.VMEM((2, total, tokens), BF16),
            pltpu.VMEM((top, total, tokens), BF16),
            pltpu.VMEM((3, total, 1), F32),
            pltpu.VMEM((2 * total, FF), BF16),
            pltpu.VMEM((2 * total, FF), BF16),
            pltpu.VMEM((half, total, part), BF16),
            pltpu.VMEM((half, total, part), BF16),
            pltpu.VMEM((T, total, part), BF16),
            pltpu.VMEM((T, total, part), BF16),
            pltpu.VMEM((T, total, part), BF16),
            pltpu.VMEM((total, part), F32),
            pltpu.VMEM((total, part), BF16),
            pltpu.VMEM((total, part), BF16),
            pltpu.VMEM((2, part, NT), BF16),
            pltpu.VMEM((2, NT, part), BF16),
            dma((3,)),
            dma((4,)),
            dma((3 * T,)),
            dma((3 * T,)),
            dma((3 * T,)),
            dma((3 * T,)),
            dma((3 * T,)),
            dma((2 * half,)),
            dma((2 * half,)),
            dma((2,)),
            dma((2,)),
            dma((T,)),
            dma((T,)),
            dma((T,)),
            dma((T,)),
            dma((2,)),
            dma((2,)),
            dma((2,)),
        ],
        compiler_params=pltpu.CompilerParams(
            collective_id=0, has_side_effects=True, vmem_limit_bytes=67043328
        ),
    )(
        routes_real.T,
        gates_real.T,
        routes_fake.T,
        gates_fake.T,
        x_real,
        x_fake,
        cotangent,
        up_real,
        down_real,
        up_fake,
        down_fake,
    )


def solution(mesh):
    in_specs = (
        P(("expert", "dp"), "tensor"),
        P(("expert", "dp"), None),
        P(("expert", "dp"), None),
        P("expert", None, "tensor"),
        P("expert", "tensor", None),
        P(("expert", "dp"), "tensor"),
        P(("expert", "dp"), None),
        P(("expert", "dp"), None),
        P(("expert", "dp"), "tensor"),
        P("expert", None, "tensor"),
        P("expert", "tensor", None),
    )
    out_specs = (
        P(("expert", "dp"), "tensor"),
        P("expert", "dp", "tensor"),
        P("expert", "tensor", "dp"),
    )
    return jax.shard_map(
        on_device, mesh=mesh, in_specs=in_specs, out_specs=out_specs, check_vma=False
    )
```

profile of v0, /device:TPU:0, one launch (start us, length us, event | category | flops | bytes accessed | tf_op | source)
XLA Modules:
  0.0 123.8 jit_solution(1096040765395708646)
XLA Ops:
  0.6 114.5 %moe.1 = (bf16[256,512]{1,0:T(8,128)(2,1)}, bf16[1,1024,2048]{2,1,0:T(8,128)(2,1)}, bf16[1,2048,1024]{2,1,0:T(8,128)(2,1)}) custom-call(s32[2,256]{1,0:T(2,128)} %bitcast.4, f32[2,256]{1,0:T(2,128)} %bitcast.5, s32[2,256]{1,0:T(2,128)} %bitcast.6, f32[2,256]{1,0:T(2,128)} %bitcast.7, bf16[256,512]{1,0:T(8,128)(2,1)} %x_real.1, bf16[256,512]{1,0:T(8,128)(2,1)} %x_fake.1, ...), custom_call_target="tpu_custom_call" | custom-call | tf_op jit(solution)/shard_map/moe/pallas_call | solution.py:614
  115.2 0.0 copy-start
  115.2 1.8 %copy.17 = bf16[256,512]{1,0:T(8,128)(2,1)} copy(bf16[256,512]{1,0:T(8,128)(2,1)} %get-tuple-element.6) | data formatting | bytes 524288
  117.0 4.8 %copy.18 = bf16[1,1024,2048]{2,1,0:T(8,128)(2,1)} copy(bf16[1,1024,2048]{2,1,0:T(8,128)(2,1)} %get-tuple-element.7) | data formatting | bytes 8388608
  121.8 0.0 copy-done
  121.8 2.0 %copy.19 = bf16[1,2048,1024]{2,1,0:T(8,128)(2,1)} copy(bf16[1,2048,1024]{2,1,0:T(8,128)(2,1)S(1)} %copy-done) | data formatting | bytes 8388608
Async XLA Ops:
  115.2 6.6 %copy-start = (bf16[1,2048,1024]{2,1,0:T(8,128)(2,1)S(1)}, bf16[1,2048,1024]{2,1,0:T(8,128)(2,1)}, u32[]{:S(2)}) copy-start(bf16[1,2048,1024]{2,1,0:T(8,128)(2,1)} %get-tuple-element.8) | copy-start | bytes 12582916
where the time goes:
time: 124 us
  Pallas kernels  115 us (93%)
  local copies, waits for them, and re-layouts  8.62 us (7%)
    pallas_call x1, Pallas kernels, on_device(): pl.pallas_call(functools.partial(moe_kernel, E, T), name='moe', out_shape...  115 us
    unnamed x5, local copies, waits for them, and re-layouts  8.62 us

commit v1 on v0

--- a/solution.py
+++ b/solution.py
@@ -12,7 +12,8 @@
 MESH = pl.DeviceIdType.MESH
 F32 = jnp.float32
 BF16 = jnp.bfloat16
-LAG = 2
+LAG = 3
+CUTS = 2
 
 
 def dot32(left, right, dims=((1,), (0,))):
@@ -48,7 +49,8 @@
     up_fake,
     down_fake,
     real_out,
-    grad_up,
+    x_up,
+    d_up,
     grad_down,
     whole,
     sendbuf,
@@ -62,7 +64,7 @@
     gate,
     act,
     dpre,
-    other_x,
+    x_turned,
     other_d,
     partial,
     from_left,
@@ -70,7 +72,6 @@
     final,
     ret_send,
     returned,
-    stage_up,
     stage_down,
     in_sem,
     w_sem,
@@ -79,16 +80,20 @@
     z_left,
     x_send,
     x_recv,
+    xt_keep,
+    xt_send,
+    xt_recv,
     d_send,
     d_recv,
-    big_send,
-    big_recv,
+    act_sems,
+    dp_keep,
+    dp_send,
+    dp_recv,
     rsr_send,
     rsr_recv,
     rsl_send,
     rsl_recv,
     ret_sems,
-    up_sem,
     down_sem,
 ):
     E, T = experts, tensors
@@ -97,7 +102,7 @@
     total = E * cap
     part = x_real.shape[1]
     FF = act.shape[1]
-    NT = stage_up.shape[2]
+    NT = stage_down.shape[1]
     tiles = FF // NT
     half = T // 2
     e = lax.axis_index("expert")
@@ -128,19 +133,17 @@
     def load(src, dst, k):
         return pltpu.make_async_copy(src.at[0], dst, w_sem.at[k])
 
-    load(up_real, weight0, 0).start()
-    load(down_real, weight1, 1).start()
-
     pl.semaphore_wait(barrier, E + jnp.minimum(t, 1) + jnp.minimum(last - t, 1))
 
-    def z_copy(i, q, right):
-        a = i // T
-        k = a * T + q
-        return pltpu.make_async_remote_copy(
-            src_ref=whole.at[k],
-            dst_ref=whole.at[k],
-            send_sem=(z_right if right else z_left).at[k],
-            recv_sem=z_recv.at[k],
+    piece = tokens // CUTS
+
+    def z_copy(i, q, cut, right):
+        k = (i // T) * T + q
+        return pltpu.make_async_remote_copy(
+            src_ref=whole.at[k, pl.ds(cut * piece, piece)],
+            dst_ref=whole.at[k, pl.ds(cut * piece, piece)],
+            send_sem=(z_right if right else z_left).at[k, cut],
+            recv_sem=z_recv.at[k, cut],
             device_id={"tensor": t + 1 if right else t - 1},
             device_id_type=MESH,
         )
@@ -153,20 +156,39 @@
         beyond = jnp.where(t < last - t, t + p - near, t - p + near)
         return jnp.where(p <= 2 * near, close, beyond)
 
+    at_end = jnp.logical_or(t == 0, t == last)
+
+    def send_own(i):
+        for cut in range(CUTS):
+
+            @pl.when(t < last)
+            def _():
+                z_copy(i, t, cut, True).start()
+
+            @pl.when(t > 0)
+            def _():
+                z_copy(i, t, cut, False).start()
+
     def gather_step(i):
         q = source(i % T)
 
-        @pl.when(q != t)
-        def _():
-            z_copy(i, q, True).wait_recv()
-
-        @pl.when(jnp.logical_and(q <= t, t < last))
-        def _():
-            z_copy(i, q, True).start()
-
-        @pl.when(jnp.logical_and(q >= t, t > 0))
-        def _():
-            z_copy(i, q, False).start()
+        @pl.when(jnp.logical_and(q == t, jnp.logical_not(at_end)))
+        def _():
+            send_own(i)
+
+        for cut in range(CUTS):
+
+            @pl.when(q != t)
+            def _():
+                z_copy(i, q, cut, True).wait_recv()
+
+            @pl.when(jnp.logical_and(q < t, t < last))
+            def _():
+                z_copy(i, q, cut, True).start()
+
+            @pl.when(jnp.logical_and(q > t, t > 0))
+            def _():
+                z_copy(i, q, cut, False).start()
 
     def x_copies(k):
         return [
@@ -201,12 +223,26 @@
         for copy in x_copies(k):
             copy.start()
 
+    inner = jnp.logical_not(at_end)
+
     def feed(i):
-        gather_step(i)
+        @pl.when(at_end)
+        def _():
+            gather_step(i)
+
         dispatch_step(i)
 
     own_in[0].wait()
-    gather_step(0)
+    send_own(0)
+    own_in[1].wait()
+    own_in[2].wait()
+
+    @pl.when(at_end)
+    def _():
+        send_own(T)
+        send_own(2 * T)
+
+    load(up_real, weight0, 0).start()
 
     square = (tokens, tokens)
     down_at = lax.broadcasted_iota(jnp.int32, square, 0)
@@ -250,10 +286,14 @@
         gated = jnp.where(mask, gates_fake[k : k + 1, :], gated)
     pick[1] = chosen
     gate[2] = jnp.sum(gated, axis=1, keepdims=True)
-    own_in[1].wait()
-    own_in[2].wait()
     for i in range(1, LAG):
-        feed(jnp.int32(i))
+        gather_step(jnp.int32(i))
+        dispatch_step(jnp.int32(i))
+
+    @pl.when(inner)
+    def _():
+        gather_step(jnp.int32(LAG))
+
 
     def tile_at(n):
         return pl.ds(pl.multiple_of(n * NT, NT), NT)
@@ -267,6 +307,7 @@
             target[:, tile_at(n)] = jnp.zeros((total, NT), F32)
 
     clear(acc0)
+    load(down_real, weight1, 1).start()
     load(up_real, weight0, 0).wait()
 
     @pl.loop(0, T)
@@ -280,20 +321,16 @@
 
         feed(p + LAG)
 
+        @pl.when(inner)
+        def _():
+            gather_step(p + LAG + 1)
+
     load(up_fake, weight0, 2).start()
 
     @pl.loop(0, tiles)
     def _(n):
         value = acc0[:, tile_at(n)]
-        dpre[0:total, tile_at(n)] = gelu_from(value, tanh_of(value)).astype(BF16)
-
-    load(down_real, weight1, 1).wait()
-
-    @pl.loop(0, T)
-    def _(c):
-        partial[c] = dot32(dpre[0:total], weight1[:, part_at(c)]).astype(BF16)
-
-    load(down_fake, weight1, 3).start()
+        dpre[:, tile_at(n)] = gelu_from(value, tanh_of(value)).astype(BF16)
 
     def rs_right(c, first):
         return pltpu.make_async_remote_copy(
@@ -393,23 +430,77 @@
         def _():
             rs_round(h)
 
-        @pl.when(j == 2 * last)
+        @pl.when(j == 2 * last + 1)
         def _():
             rs_final()
 
-    rs_round(jnp.int32(0))
+    load(down_real, weight1, 1).wait()
+
+    @pl.loop(0, T)
+    def _(k):
+        c = jnp.where(t < half, last - k, k)
+        partial[c] = dot32(dpre[...], weight1[:, part_at(c)]).astype(BF16)
+
+        @pl.when(k == 0)
+        def _():
+            rs_round(jnp.int32(0))
+
+        @pl.when(jnp.logical_and(inner, k < 2))
+        def _():
+            gather_step(T + LAG + 1 + k)
+
+    load(down_fake, weight1, 3).start()
 
     def half_of(q):
         return q // half
 
-    def swap(a, q, target):
-        k = a * T + q
+    base = d * half
+
+    def swap(q):
         other = q - (1 - d) * half
         return pltpu.make_async_remote_copy(
-            src_ref=rows.at[k],
-            dst_ref=target.at[other],
-            send_sem=d_send.at[(a - 1) * half + other],
-            recv_sem=d_recv.at[(a - 1) * half + other],
+            src_ref=rows.at[2 * T + q],
+            dst_ref=other_d.at[other],
+            send_sem=d_send.at[other],
+            recv_sem=d_recv.at[other],
+            device_id={"dp": 1 - d},
+            device_id_type=MESH,
+        )
+
+    def swap_in(j):
+        return pltpu.make_async_remote_copy(
+            src_ref=rows.at[2 * T + j],
+            dst_ref=other_d.at[j],
+            send_sem=d_send.at[j],
+            recv_sem=d_recv.at[j],
+            device_id={"dp": 1 - d},
+            device_id_type=MESH,
+        )
+
+    def turned_keep(q):
+        return pltpu.make_async_copy(
+            x_turned.at[q],
+            x_up.at[pl.ds((q - base) * part, part), pl.ds(0, total)],
+            xt_keep.at[q - base],
+        )
+
+    def turned_send(q):
+        other = q - (1 - d) * half
+        return pltpu.make_async_remote_copy(
+            src_ref=x_turned.at[q],
+            dst_ref=x_up.at[pl.ds(other * part, part), pl.ds(total, total)],
+            send_sem=xt_send.at[other],
+            recv_sem=xt_recv.at[other],
+            device_id={"dp": 1 - d},
+            device_id_type=MESH,
+        )
+
+    def turned_in(j):
+        return pltpu.make_async_remote_copy(
+            src_ref=x_turned.at[j],
+            dst_ref=x_up.at[pl.ds(j * part, part), pl.ds(total, total)],
+            send_sem=xt_send.at[j],
+            recv_sem=xt_recv.at[j],
             device_id={"dp": 1 - d},
             device_id_type=MESH,
         )
@@ -422,16 +513,26 @@
         q = source(p)
         x_all(T + q).wait_recv()
 
-        @pl.when(half_of(q) != d)
-        def _():
-            swap(1, q, other_x).start()
-
         @pl.loop(0, tiles)
         def _(n):
             acc1[:, tile_at(n)] += dot32(rows[T + q], weight0[part_at(q), tile_at(n)])
 
         feed(T + p + LAG)
         rs_slot(p)
+
+        @pl.when(jnp.logical_and(inner, p + LAG + 3 < 2 * T))
+        def _():
+            gather_step(T + p + LAG + 3)
+
+        x_turned[q] = rows[T + q].T
+
+        @pl.when(half_of(q) == d)
+        def _():
+            turned_keep(q).start()
+
+        @pl.when(half_of(q) != d)
+        def _():
+            turned_send(q).start()
 
     @pl.loop(0, tiles)
     def _(n):
@@ -440,28 +541,72 @@
         act[0:total, tile_at(n)] = gelu_from(value, inner).astype(BF16)
         acc1[:, tile_at(n)] = slope_from(value, inner)
 
-    def across(buffer, k):
-        return pltpu.make_async_remote_copy(
-            src_ref=buffer.at[pl.ds(0, total)],
-            dst_ref=buffer.at[pl.ds(total, total)],
-            send_sem=big_send.at[k],
-            recv_sem=big_recv.at[k],
+    def act_across():
+        return pltpu.make_async_remote_copy(
+            src_ref=act.at[pl.ds(0, total)],
+            dst_ref=act.at[pl.ds(total, total)],
+            send_sem=act_sems.at[0],
+            recv_sem=act_sems.at[1],
             device_id={"dp": 1 - d},
             device_id_type=MESH,
         )
 
+    def dpre_keep(n):
+        return pltpu.make_async_copy(
+            dpre.at[:, tile_at(n)], d_up.at[pl.ds(0, total), tile_at(n)], dp_keep.at[n]
+        )
+
+    def dpre_across(n):
+        return pltpu.make_async_remote_copy(
+            src_ref=dpre.at[:, tile_at(n)],
+            dst_ref=d_up.at[pl.ds(total, total), tile_at(n)],
+            send_sem=dp_send.at[n],
+            recv_sem=dp_recv.at[n],
+            device_id={"dp": 1 - d},
+            device_id_type=MESH,
+        )
+
+    def put_down(j, n):
+        return pltpu.make_async_copy(
+            stage_down.at[n], grad_down.at[tile_at(n), part_at(j)], down_sem.at[n]
+        )
+
+    first_down = jnp.clip(t, base, base + half - 1)
+
+    def down_step(q):
+        @pl.when(half_of(q) == d)
+        def _():
+            j = q - base
+            swap_in(j).wait_recv()
+
+            @pl.loop(0, tiles)
+            def _(n):
+                @pl.when(q != first_down)
+                def _():
+                    put_down(j, n).wait()
+
+                tile = dot32(act[0:total, tile_at(n)], rows[2 * T + q], ((0,), (0,)))
+                tile = tile + dot32(
+                    act[total : 2 * total, tile_at(n)], other_d[j], ((0,), (0,))
+                )
+                stage_down[n] = tile.astype(BF16)
+                put_down(j, n).start()
+
     clear(acc0)
-    across(act, 0).start()
+    act_across().start()
     load(down_fake, weight1, 3).wait()
 
-    @pl.loop(0, T)
+    def take_rows(q):
+        x_all(2 * T + q).wait_recv()
+
+        @pl.when(half_of(q) != d)
+        def _():
+            swap(q).start()
+
+    @pl.loop(0, last)
     def _(p):
         q = source(p)
-        x_all(2 * T + q).wait_recv()
-
-        @pl.when(half_of(q) != d)
-        def _():
-            swap(2, q, other_d).start()
+        take_rows(q)
 
         @pl.loop(0, tiles)
         def _(n):
@@ -473,73 +618,35 @@
         def _():
             feed(2 * T + p + LAG)
 
+        @pl.when(jnp.logical_and(inner, p + LAG + 3 < T))
+        def _():
+            gather_step(2 * T + p + LAG + 3)
+
         rs_slot(T + p)
+
+        @pl.when(p == 0)
+        def _():
+            act_across().wait_recv()
+
+        @pl.when(p > 0)
+        def _():
+            down_step(source(p - 1))
+
+    q_last = source(last)
+    take_rows(q_last)
 
     @pl.loop(0, tiles)
     def _(n):
-        dpre[0:total, tile_at(n)] = (acc0[:, tile_at(n)] * acc1[:, tile_at(n)]).astype(BF16)
-
-    across(dpre, 1).start()
-
-    def other_in(a, j, target):
-        return pltpu.make_async_remote_copy(
-            src_ref=rows.at[a * T + j],
-            dst_ref=target.at[j],
-            send_sem=d_send.at[(a - 1) * half + j],
-            recv_sem=d_recv.at[(a - 1) * half + j],
-            device_id={"dp": 1 - d},
-            device_id_type=MESH,
-        )
-
-    @pl.loop(0, half)
-    def _(j):
-        other_in(1, j, other_x).wait_recv()
-        other_in(2, j, other_d).wait_recv()
-
-    across(act, 0).wait_recv()
-    base = d * half
-
-    def put_down(j, n):
-        slot = (j * tiles + n) % 2
-        return pltpu.make_async_copy(
-            stage_down.at[slot], grad_down.at[0, tile_at(n), part_at(j)], down_sem.at[slot]
-        )
-
-    def put_up(j, n):
-        slot = (j * tiles + n) % 2
-        return pltpu.make_async_copy(
-            stage_up.at[slot], grad_up.at[0, part_at(j), tile_at(n)], up_sem.at[slot]
-        )
-
-    @pl.loop(0, half * tiles)
-    def _(w):
-        j = w // tiles
-        n = w % tiles
-
-        @pl.when(w >= 2)
-        def _():
-            put_down(j, n).wait()
-
-        tile = dot32(act[0:total, tile_at(n)], rows[2 * T + base + j], ((0,), (0,)))
-        tile = tile + dot32(act[total : 2 * total, tile_at(n)], other_d[j], ((0,), (0,)))
-        stage_down[w % 2] = tile.astype(BF16)
-        put_down(j, n).start()
-
-    across(dpre, 1).wait_recv()
-
-    @pl.loop(0, half * tiles)
-    def _(w):
-        j = w // tiles
-        n = w % tiles
-
-        @pl.when(w >= 2)
-        def _():
-            put_up(j, n).wait()
-
-        tile = dot32(rows[T + base + j], dpre[0:total, tile_at(n)], ((0,), (0,)))
-        tile = tile + dot32(other_x[j], dpre[total : 2 * total, tile_at(n)], ((0,), (0,)))
-        stage_up[w % 2] = tile.astype(BF16)
-        put_up(j, n).start()
+        back = acc0[:, tile_at(n)] + dot32(
+            rows[2 * T + q_last], weight1[tile_at(n), part_at(q_last)], ((1,), (1,))
+        )
+        dpre[:, tile_at(n)] = (back * acc1[:, tile_at(n)]).astype(BF16)
+        dpre_across(n).start()
+        dpre_keep(n).start()
+
+    rs_slot(T + last)
+    down_step(source(last - 1))
+    down_step(q_last)
 
     ret_all().wait_recv()
     out = jnp.zeros((tokens, part), F32)
@@ -548,30 +655,34 @@
         out = out + stand_up(gates_real[k : k + 1, :]) * back
     real_out[...] = out.astype(BF16)
 
-    for w in range(max(0, half * tiles - 2), half * tiles):
-        put_down(w // tiles, w % tiles).wait()
-        put_up(w // tiles, w % tiles).wait()
+    @pl.loop(0, tiles)
+    def _(n):
+        put_down(0, n).wait()
+        dpre_across(n).wait()
+        dpre_keep(n).wait()
+
+    @pl.loop(0, half)
+    def _(j):
+        turned_in(j).wait()
+        turned_keep(base + j).wait()
+        swap_in(j).wait_send()
+
+    act_across().wait_send()
 
     @pl.loop(0, 3 * T)
     def _(k):
         x_all(k).wait_send()
         q = k % T
-
-        @pl.when(jnp.logical_and(q <= t, t < last))
-        def _():
-            z_copy(k, q, True).wait_send()
-
-        @pl.when(jnp.logical_and(q >= t, t > 0))
-        def _():
-            z_copy(k, q, False).wait_send()
-
-    @pl.loop(0, half)
-    def _(j):
-        other_in(1, j, other_x).wait_send()
-        other_in(2, j, other_d).wait_send()
-
-    across(act, 0).wait_send()
-    across(dpre, 1).wait_send()
+        for cut in range(CUTS):
+
+            @pl.when(jnp.logical_and(q <= t, t < last))
+            def _():
+                z_copy(k, q, cut, True).wait_send()
+
+            @pl.when(jnp.logical_and(q >= t, t > 0))
+            def _():
+                z_copy(k, q, cut, False).wait_send()
+
     ret_all().wait_send()
 
     @pl.loop(0, T)
@@ -583,6 +694,75 @@
         @pl.when(c < t)
         def _():
             rs_left(c, False).wait_send()
+
+
+def up_kernel(
+    x_up,
+    d_up,
+    down_in,
+    real_in,
+    grad_up,
+    grad_down,
+    real_out,
+    left,
+    right,
+    done,
+    passed,
+    small,
+    sem_left,
+    sem_in,
+    sem_out,
+    sem_down_in,
+    sem_down_out,
+    sem_small,
+):
+    steps, _, wide = right.shape
+    tall = passed.shape[1]
+
+    def columns(n):
+        return pl.ds(n * wide, wide)
+
+    def lines(n):
+        return pl.ds(n * tall, tall)
+
+    lefts = pltpu.make_async_copy(x_up, left, sem_left)
+    ins = [
+        pltpu.make_async_copy(d_up.at[:, columns(n)], right.at[n], sem_in.at[n])
+        for n in range(steps)
+    ]
+    outs = [
+        pltpu.make_async_copy(done.at[n], grad_up.at[:, columns(n)], sem_out.at[n])
+        for n in range(steps)
+    ]
+    down_ins = [
+        pltpu.make_async_copy(down_in.at[lines(n)], passed.at[n], sem_down_in.at[n])
+        for n in range(steps)
+    ]
+    down_outs = [
+        pltpu.make_async_copy(passed.at[n], grad_down.at[lines(n)], sem_down_out.at[n])
+        for n in range(steps)
+    ]
+    small_in = pltpu.make_async_copy(real_in, small, sem_small.at[0])
+    small_out = pltpu.make_async_copy(small, real_out, sem_small.at[1])
+    lefts.start()
+    for n in range(steps):
+        ins[n].start()
+    small_in.start()
+    for n in range(steps):
+        down_ins[n].start()
+    lefts.wait()
+    for n in range(steps):
+        ins[n].wait()
+        done[n] = dot32(left[...], right[n]).astype(BF16)
+        outs[n].start()
+        down_ins[n].wait()
+        down_outs[n].start()
+    small_in.wait()
+    small_out.start()
+    for n in range(steps):
+        outs[n].wait()
+        down_outs[n].wait()
+    small_out.wait()
 
 
 def on_device(
@@ -611,16 +791,17 @@
     vmem = pl.BlockSpec(memory_space=pltpu.VMEM)
     hbm = pl.BlockSpec(memory_space=pl.ANY)
     dma = pltpu.SemaphoreType.DMA
-    return pl.pallas_call(
+    real_out, x_up, d_up, grad_down = pl.pallas_call(
         functools.partial(moe_kernel, E, T),
         name="moe",
         out_shape=(
             jax.ShapeDtypeStruct((tokens, part), BF16),
-            jax.ShapeDtypeStruct((1, D // 2, FF), BF16),
-            jax.ShapeDtypeStruct((1, FF, D // 2), BF16),
+            jax.ShapeDtypeStruct((D // 2, 2 * total), BF16),
+            jax.ShapeDtypeStruct((2 * total, FF), BF16),
+            jax.ShapeDtypeStruct((FF, D // 2), BF16),
         ),
         in_specs=[vmem] * 4 + [hbm] * 7,
-        out_specs=(vmem, hbm, hbm),
+        out_specs=(vmem, hbm, hbm, hbm),
         scratch_shapes=[
             pltpu.VMEM((3 * T, tokens, part), BF16),
             pltpu.VMEM((3 * T, total - cap, part), BF16),
@@ -633,8 +814,8 @@
             pltpu.VMEM((top, total, tokens), BF16),
             pltpu.VMEM((3, total, 1), F32),
             pltpu.VMEM((2 * total, FF), BF16),
-            pltpu.VMEM((2 * total, FF), BF16),
-            pltpu.VMEM((half, total, part), BF16),
+            pltpu.VMEM((total, FF), BF16),
+            pltpu.VMEM((T, part, total), BF16),
             pltpu.VMEM((half, total, part), BF16),
             pltpu.VMEM((T, total, part), BF16),
             pltpu.VMEM((T, total, part), BF16),
@@ -642,26 +823,29 @@
             pltpu.VMEM((total, part), F32),
             pltpu.VMEM((total, part), BF16),
             pltpu.VMEM((total, part), BF16),
-            pltpu.VMEM((2, part, NT), BF16),
-            pltpu.VMEM((2, NT, part), BF16),
+            pltpu.VMEM((FF // NT, NT, part), BF16),
             dma((3,)),
             dma((4,)),
+            dma((3 * T, CUTS)),
+            dma((3 * T, CUTS)),
+            dma((3 * T, CUTS)),
             dma((3 * T,)),
             dma((3 * T,)),
-            dma((3 * T,)),
-            dma((3 * T,)),
-            dma((3 * T,)),
-            dma((2 * half,)),
-            dma((2 * half,)),
+            dma((half,)),
+            dma((half,)),
+            dma((half,)),
+            dma((half,)),
+            dma((half,)),
             dma((2,)),
-            dma((2,)),
+            dma((FF // NT,)),
+            dma((FF // NT,)),
+            dma((FF // NT,)),
             dma((T,)),
             dma((T,)),
             dma((T,)),
             dma((T,)),
             dma((2,)),
-            dma((2,)),
-            dma((2,)),
+            dma((FF // NT,)),
         ],
         compiler_params=pltpu.CompilerParams(
             collective_id=0, has_side_effects=True, vmem_limit_bytes=67043328
@@ -679,6 +863,34 @@
         up_fake,
         down_fake,
     )
+    steps = 4
+    wide = FF // steps
+    grad_up, grad_down, real_out = pl.pallas_call(
+        up_kernel,
+        name="finish",
+        out_shape=(
+            jax.ShapeDtypeStruct((D // 2, FF), BF16),
+            jax.ShapeDtypeStruct((FF, D // 2), BF16),
+            jax.ShapeDtypeStruct((tokens, part), BF16),
+        ),
+        in_specs=[hbm] * 4,
+        out_specs=(hbm,) * 3,
+        scratch_shapes=[
+            pltpu.VMEM((D // 2, 2 * total), BF16),
+            pltpu.VMEM((steps, 2 * total, wide), BF16),
+            pltpu.VMEM((steps, D // 2, wide), BF16),
+            pltpu.VMEM((steps, wide, D // 2), BF16),
+            pltpu.VMEM((tokens, part), BF16),
+            dma(()),
+            dma((steps,)),
+            dma((steps,)),
+            dma((steps,)),
+            dma((steps,)),
+            dma((2,)),
+        ],
+        compiler_params=pltpu.CompilerParams(vmem_limit_bytes=67043328),
+    )(x_up, d_up, grad_down, real_out)
+    return real_out, grad_up[None], grad_down[None]
 
 
 def solution(mesh):

time: 124 us -> 101 us (0.81)
  Pallas kernels: 115 us -> 100 us
  local copies, waits for them, and re-layouts: 8.62 us -> 0 us
    pallas_call x1, Pallas kernels: 115 us -> 90.3 us  [on_device(): pl.pallas_call(functools.partial(moe_kernel, E, T), name='moe', out_shape...]
    pallas_call x0 -> x1, Pallas kernels: none -> 10 us  [on_device(): pl.pallas_call(up_kernel, name='finish', out_shape=(jax.ShapeDtypeStruct(...]
    unnamed x5 -> x0, local copies, waits for them, and re-layouts: 8.62 us -> none
where the time goes in v1:
time: 101 us
  Pallas kernels  100 us (99%)
    pallas_call x1, Pallas kernels, on_device(): pl.pallas_call(functools.partial(moe_kernel, E, T), name='moe', out_shape...  90.3 us
    pallas_call x1, Pallas kernels, on_device(): pl.pallas_call(up_kernel, name='finish', out_shape=(jax.ShapeDtypeStruct(...  10 us

profile of v1, /device:TPU:0, one launch (start us, length us, event | category | flops | bytes accessed | tf_op | source)
XLA Modules:
  0.0 101.1 jit_solution(6410683529245435517)
XLA Ops:
  0.6 90.3 %moe.1 = (bf16[256,512]{1,0:T(8,128)(2,1)}, bf16[1024,1024]{1,0:T(8,128)(2,1)}, bf16[1024,2048]{1,0:T(8,128)(2,1)}, bf16[2048,1024]{1,0:T(8,128)(2,1)}) custom-call(s32[2,256]{1,0:T(2,128)} %bitcast.6, f32[2,256]{1,0:T(2,128)} %bitcast.7, s32[2,256]{1,0:T(2,128)} %bitcast.8, f32[2,256]{1,0:T(2,128)} %bitcast.9, bf16[256,512]{1,0:T(8,128)(2,1)} %x_real.1, ...), custom_call_target="tpu_custom_call" | custom-call | tf_op jit(solution)/shard_map/moe/pallas_call | solution.py:794
  90.9 10.0 %finish.1 = (bf16[1024,2048]{1,0:T(8,128)(2,1)}, bf16[2048,1024]{1,0:T(8,128)(2,1)}, bf16[256,512]{1,0:T(8,128)(2,1)}) custom-call(bf16[1024,1024]{1,0:T(8,128)(2,1)} %get-tuple-element.10.x_up, bf16[1024,2048]{1,0:T(8,128)(2,1)} %get-tuple-element.11.d_up, bf16[2048,1024]{1,0:T(8,128)(2,1)} %get-tuple-element.12.down_in, ...), custom_call_target="tpu_custom_call" | custom-call | tf_op jit(solution)/shard_map/finish/pallas_call | solution.py:868

commit v2 on v1

--- a/solution.py
+++ b/solution.py
@@ -73,7 +73,9 @@
     ret_send,
     returned,
     stage_down,
+    final_out,
     in_sem,
+    out_sem,
     w_sem,
     z_recv,
     z_right,
@@ -133,6 +135,41 @@
     def load(src, dst, k):
         return pltpu.make_async_copy(src.at[0], dst, w_sem.at[k])
 
+    square = (tokens, tokens)
+    down_at = lax.broadcasted_iota(jnp.int32, square, 0)
+    along = lax.broadcasted_iota(jnp.int32, square, 1)
+    eye = down_at == along
+    upper = (down_at < along).astype(BF16)
+    labels_high = max(8, E)
+    labels = lax.broadcasted_iota(jnp.int32, (labels_high, tokens), 0).astype(F32)
+    slot_rows = lax.broadcasted_iota(jnp.int32, (total, tokens), 0).astype(F32)
+
+    def stand_up(row):
+        return jnp.sum(jnp.where(eye, row, 0.0), axis=1, keepdims=True)
+
+    def positions(routes):
+        names = [routes[k : k + 1, :].astype(F32) for k in range(top)]
+        places = [(routes[k : k + 1, :] ^ e).astype(F32) for k in range(top)]
+        hits = jnp.zeros((labels_high, tokens), F32)
+        for name in names:
+            hits = hits + (labels == name).astype(F32)
+        before = dot32(hits.astype(BF16), upper)
+        found = []
+        for name, place in zip(names, places):
+            slot = jnp.sum(jnp.where(labels == name, before, 0.0), axis=0, keepdims=True)
+            found.append(place * cap + slot)
+        return found
+
+    chosen = jnp.zeros((total, tokens), BF16)
+    for k, where in enumerate(positions(routes_real)):
+        mask = (slot_rows == where).astype(F32).astype(BF16)
+        pick_k[k] = mask
+        chosen = chosen + mask
+    pick[0] = chosen
+    gate[0] = jnp.ones((total, 1), F32)
+    for copy in own_in:
+        copy.wait()
+
     pl.semaphore_wait(barrier, E + jnp.minimum(t, 1) + jnp.minimum(last - t, 1))
 
     piece = tokens // CUTS
@@ -150,9 +187,10 @@
 
     near = jnp.minimum(t, last - t)
 
-    def source(p):
+    def source(p, a):
         step = (p + 1) // 2
-        close = jnp.where(p % 2 == 1, t - step, t + step)
+        side = jnp.where(jnp.logical_xor(t < half, a == 0), -1, 1)
+        close = t + jnp.where(p % 2 == 1, side, -side) * step
         beyond = jnp.where(t < last - t, t + p - near, t - p + near)
         return jnp.where(p <= 2 * near, close, beyond)
 
@@ -170,7 +208,7 @@
                 z_copy(i, t, cut, False).start()
 
     def gather_step(i):
-        q = source(i % T)
+        q = source(i % T, i // T)
 
         @pl.when(jnp.logical_and(q == t, jnp.logical_not(at_end)))
         def _():
@@ -215,7 +253,7 @@
 
     def dispatch_step(i):
         a = i // T
-        k = a * T + source(i % T)
+        k = a * T + source(i % T, a)
         which = jnp.minimum(a, 1)
         picked = (dot32(pick[which], whole[k]) * gate[a]).astype(BF16)
         rows[k, 0:cap] = picked[0:cap]
@@ -232,10 +270,7 @@
 
         dispatch_step(i)
 
-    own_in[0].wait()
     send_own(0)
-    own_in[1].wait()
-    own_in[2].wait()
 
     @pl.when(at_end)
     def _():
@@ -244,38 +279,6 @@
 
     load(up_real, weight0, 0).start()
 
-    square = (tokens, tokens)
-    down_at = lax.broadcasted_iota(jnp.int32, square, 0)
-    along = lax.broadcasted_iota(jnp.int32, square, 1)
-    eye = down_at == along
-    upper = (down_at < along).astype(BF16)
-    labels_high = max(8, E)
-    labels = lax.broadcasted_iota(jnp.int32, (labels_high, tokens), 0).astype(F32)
-    slot_rows = lax.broadcasted_iota(jnp.int32, (total, tokens), 0).astype(F32)
-
-    def stand_up(row):
-        return jnp.sum(jnp.where(eye, row, 0.0), axis=1, keepdims=True)
-
-    def positions(routes):
-        names = [routes[k : k + 1, :].astype(F32) for k in range(top)]
-        places = [(routes[k : k + 1, :] ^ e).astype(F32) for k in range(top)]
-        hits = jnp.zeros((labels_high, tokens), F32)
-        for name in names:
-            hits = hits + (labels == name).astype(F32)
-        before = dot32(hits.astype(BF16), upper)
-        found = []
-        for name, place in zip(names, places):
-            slot = jnp.sum(jnp.where(labels == name, before, 0.0), axis=0, keepdims=True)
-            found.append(place * cap + slot)
-        return found
-
-    chosen = jnp.zeros((total, tokens), BF16)
-    for k, where in enumerate(positions(routes_real)):
-        mask = (slot_rows == where).astype(F32).astype(BF16)
-        pick_k[k] = mask
-        chosen = chosen + mask
-    pick[0] = chosen
-    gate[0] = jnp.ones((total, 1), F32)
     dispatch_step(0)
     gate[1] = jnp.ones((total, 1), F32)
     chosen = jnp.zeros((total, tokens), BF16)
@@ -312,7 +315,7 @@
 
     @pl.loop(0, T)
     def _(p):
-        q = source(p)
+        q = source(p, 0)
         x_all(q).wait_recv()
 
         @pl.loop(0, tiles)
@@ -430,7 +433,7 @@
         def _():
             rs_round(h)
 
-        @pl.when(j == 2 * last + 1)
+        @pl.when(j == 2 * last)
         def _():
             rs_final()
 
@@ -510,7 +513,7 @@
 
     @pl.loop(0, T)
     def _(p):
-        q = source(p)
+        q = source(p, 1)
         x_all(T + q).wait_recv()
 
         @pl.loop(0, tiles)
@@ -553,13 +556,13 @@
 
     def dpre_keep(n):
         return pltpu.make_async_copy(
-            dpre.at[:, tile_at(n)], d_up.at[pl.ds(0, total), tile_at(n)], dp_keep.at[n]
+            dpre.at[:, tile_at(n)], d_up.at[n, pl.ds(0, total)], dp_keep.at[n]
         )
 
     def dpre_across(n):
         return pltpu.make_async_remote_copy(
             src_ref=dpre.at[:, tile_at(n)],
-            dst_ref=d_up.at[pl.ds(total, total), tile_at(n)],
+            dst_ref=d_up.at[n, pl.ds(total, total)],
             send_sem=dp_send.at[n],
             recv_sem=dp_recv.at[n],
             device_id={"dp": 1 - d},
@@ -605,7 +608,7 @@
 
     @pl.loop(0, last)
     def _(p):
-        q = source(p)
+        q = source(p, 2)
         take_rows(q)
 
         @pl.loop(0, tiles)
@@ -630,9 +633,9 @@
 
         @pl.when(p > 0)
         def _():
-            down_step(source(p - 1))
-
-    q_last = source(last)
+            down_step(source(p - 1, 2))
+
+    q_last = source(last, 2)
     take_rows(q_last)
 
     @pl.loop(0, tiles)
@@ -645,15 +648,41 @@
         dpre_keep(n).start()
 
     rs_slot(T + last)
-    down_step(source(last - 1))
+    down_step(source(last - 1, 2))
     down_step(q_last)
+
+    @pl.loop(0, 3 * T)
+    def _(k):
+        x_all(k).wait_send()
+        q = k % T
+        for cut in range(CUTS):
+
+            @pl.when(jnp.logical_and(q <= t, t < last))
+            def _():
+                z_copy(k, q, cut, True).wait_send()
+
+            @pl.when(jnp.logical_and(q >= t, t > 0))
+            def _():
+                z_copy(k, q, cut, False).wait_send()
+
+    @pl.loop(0, T)
+    def _(c):
+        @pl.when(c > t)
+        def _():
+            rs_right(c, False).wait_send()
+
+        @pl.when(c < t)
+        def _():
+            rs_left(c, False).wait_send()
 
     ret_all().wait_recv()
     out = jnp.zeros((tokens, part), F32)
     for k in range(top):
         back = dot32(pick_k[k], returned[...], ((0,), (0,)))
         out = out + stand_up(gates_real[k : k + 1, :]) * back
-    real_out[...] = out.astype(BF16)
+    final_out[...] = out.astype(BF16)
+    out_copy = pltpu.make_async_copy(final_out, real_out, out_sem)
+    out_copy.start()
 
     @pl.loop(0, tiles)
     def _(n):
@@ -669,31 +698,8 @@
 
     act_across().wait_send()
 
-    @pl.loop(0, 3 * T)
-    def _(k):
-        x_all(k).wait_send()
-        q = k % T
-        for cut in range(CUTS):
-
-            @pl.when(jnp.logical_and(q <= t, t < last))
-            def _():
-                z_copy(k, q, cut, True).wait_send()
-
-            @pl.when(jnp.logical_and(q >= t, t > 0))
-            def _():
-                z_copy(k, q, cut, False).wait_send()
-
     ret_all().wait_send()
-
-    @pl.loop(0, T)
-    def _(c):
-        @pl.when(c > t)
-        def _():
-            rs_right(c, False).wait_send()
-
-        @pl.when(c < t)
-        def _():
-            rs_left(c, False).wait_send()
+    out_copy.wait()
 
 
 def up_kernel(
@@ -727,7 +733,7 @@
 
     lefts = pltpu.make_async_copy(x_up, left, sem_left)
     ins = [
-        pltpu.make_async_copy(d_up.at[:, columns(n)], right.at[n], sem_in.at[n])
+        pltpu.make_async_copy(d_up.at[n], right.at[n], sem_in.at[n])
         for n in range(steps)
     ]
     outs = [
@@ -745,18 +751,20 @@
     small_in = pltpu.make_async_copy(real_in, small, sem_small.at[0])
     small_out = pltpu.make_async_copy(small, real_out, sem_small.at[1])
     lefts.start()
+    small_in.start()
     for n in range(steps):
         ins[n].start()
-    small_in.start()
     for n in range(steps):
         down_ins[n].start()
     lefts.wait()
     for n in range(steps):
         ins[n].wait()
-        done[n] = dot32(left[...], right[n]).astype(BF16)
-        outs[n].start()
         down_ins[n].wait()
         down_outs[n].start()
+        for m in range(2):
+            lines_up = pl.ds(m * (left.shape[0] // 2), left.shape[0] // 2)
+            done[n, lines_up] = dot32(left[lines_up], right[n]).astype(BF16)
+        outs[n].start()
     small_in.wait()
     small_out.start()
     for n in range(steps):
@@ -797,11 +805,11 @@
         out_shape=(
             jax.ShapeDtypeStruct((tokens, part), BF16),
             jax.ShapeDtypeStruct((D // 2, 2 * total), BF16),
-            jax.ShapeDtypeStruct((2 * total, FF), BF16),
+            jax.ShapeDtypeStruct((FF // NT, 2 * total, NT), BF16),
             jax.ShapeDtypeStruct((FF, D // 2), BF16),
         ),
         in_specs=[vmem] * 4 + [hbm] * 7,
-        out_specs=(vmem, hbm, hbm, hbm),
+        out_specs=(hbm,) * 4,
         scratch_shapes=[
             pltpu.VMEM((3 * T, tokens, part), BF16),
             pltpu.VMEM((3 * T, total - cap, part), BF16),
@@ -824,7 +832,9 @@
             pltpu.VMEM((total, part), BF16),
             pltpu.VMEM((total, part), BF16),
             pltpu.VMEM((FF // NT, NT, part), BF16),
+            pltpu.VMEM((tokens, part), BF16),
             dma((3,)),
+            dma(()),
             dma((4,)),
             dma((3 * T, CUTS)),
             dma((3 * T, CUTS)),
@@ -863,8 +873,8 @@
         up_fake,
         down_fake,
     )
-    steps = 4
-    wide = FF // steps
+    steps = FF // NT
+    wide = NT
     grad_up, grad_down, real_out = pl.pallas_call(
         up_kernel,
         name="finish",

time: 101 us -> 97.1 us (0.961); the launches traced: 101 us -> 95.6 us
  Pallas kernels: 100 us -> 94.8 us
    pallas_call x1, Pallas kernels: 90.3 us -> 85.1 us  [on_device(): pl.pallas_call(functools.partial(moe_kernel, E, T), name='moe', out_shape...]
where the time goes in v2:
time: 97.1 us; the launch traced here: 95.6 us
  Pallas kernels  94.8 us (98%)
    pallas_call x1, Pallas kernels, on_device(): pl.pallas_call(functools.partial(moe_kernel, E, T), name='moe', out_shape...  85.1 us
    pallas_call x1, Pallas kernels, on_device(): pl.pallas_call(up_kernel, name='finish', out_shape=(jax.ShapeDtypeStruct(...  9.69 us

profile of v2, /device:TPU:0, one launch (start us, length us, event | category | flops | bytes accessed | tf_op | source)
XLA Modules:
  0.0 95.6 jit_solution(11957056079093194669)
XLA Ops:
  0.6 85.1 %moe.1 = (bf16[256,512]{1,0:T(8,128)(2,1)}, bf16[1024,1024]{1,0:T(8,128)(2,1)}, bf16[4,1024,512]{2,1,0:T(8,128)(2,1)}, bf16[2048,1024]{1,0:T(8,128)(2,1)}) custom-call(s32[2,256]{1,0:T(2,128)} %bitcast.6, f32[2,256]{1,0:T(2,128)} %bitcast.7, s32[2,256]{1,0:T(2,128)} %bitcast.8, f32[2,256]{1,0:T(2,128)} %bitcast.9, bf16[256,512]{1,0:T(8,128)(2,1)} %x_real.1, ...), custom_call_target="tpu_custom_call" | custom-call | tf_op jit(solution)/shard_map/moe/pallas_call | solution.py:802
  85.7 9.7 %finish.1 = (bf16[1024,2048]{1,0:T(8,128)(2,1)}, bf16[2048,1024]{1,0:T(8,128)(2,1)}, bf16[256,512]{1,0:T(8,128)(2,1)}) custom-call(bf16[1024,1024]{1,0:T(8,128)(2,1)} %get-tuple-element.10.x_up, bf16[4,1024,512]{2,1,0:T(8,128)(2,1)} %get-tuple-element.11.d_up, bf16[2048,1024]{1,0:T(8,128)(2,1)} %get-tuple-element.12.down_in, ...), custom_call_target="tpu_custom_call" | custom-call | tf_op jit(solution)/shard_map/finish/pallas_call | solution.py:878
